TPU v7x, 128 devices: a 2x2x16 block of a 8x8x16 slice. The times are simulated.
128 devices in a mesh: member: 4 (over y, x), mp: 32 (over z, core).
Axes of the slice: x: 2, y: 2, z: 16, core: 2. Of those that a mesh axis runs over, the one named last changes fastest.
The devices are a block of a 8x8x16 slice.
Arguments:
- nodes: bfloat16 [8192, 4096], P(('member', 'mp')), parts along dimension 0, may hold values from -6 to 6
- norm_gain: float32 [4096], replicated, may hold values from 0.1 to 1.9
- w_in: bfloat16 [4096, 16384], P(None, 'mp'), may hold values from -0.09375 to 0.09375
- b_in: float32 [16384], P('mp'), may hold values from -3 to 3
- w_out: bfloat16 [16384, 4096], P('mp'), may hold values from -0.046875 to 0.046875
- b_out: float32 [4096], replicated, may hold values from -3 to 3
Outputs:
- updated: bfloat16 [8192, 4096], P(('member', 'mp')), parts along dimension 0
There are 4 independent parts, one for each index of `member`. A program takes and returns all parts, laid end to end along the dimension named above; an argument that names none is the same for every part. Nothing has to cross between parts.
All inputs are finite; a program needn't handle non-finite values.
Results may differ from a plain program's by a relative error of at most 0.015.
Values may be sent and summed in bfloat16 or wider, within the bound.
A program may use at most 128 MiB of HBM per device.

v0:
```python
import jax
import jax.numpy as jnp
from jax import lax
from jax.sharding import PartitionSpec as P


def normalize(rows, norm_gain):
    values = rows.astype(jnp.float32)
    mean = jnp.mean(values, axis=1, keepdims=True)
    var = jnp.mean((values - mean) ** 2, axis=1, keepdims=True)
    return ((values - mean) / jnp.sqrt(var + 1e-05) * norm_gain).astype(jnp.bfloat16)


def local(nodes, norm_gain, w_in, b_in, w_out, b_out):
    source = normalize(nodes, norm_gain)
    pre = (
        jnp.dot(
            lax.all_gather(source, "mp", axis=0, tiled=True),
            w_in,
            preferred_element_type=jnp.float32,
        )
        + b_in
    )
    gathered = jax.nn.gelu(pre, approximate=True).astype(jnp.bfloat16)
    summed = lax.psum_scatter(
        jnp.dot(gathered, w_out, preferred_element_type=jnp.float32).astype(jnp.bfloat16),
        "mp",
        scatter_dimension=0,
        tiled=True,
    ).astype(jnp.float32)
    return (nodes.astype(jnp.float32) + summed + b_out).astype(jnp.bfloat16)


def solution(mesh):
    return jax.shard_map(
        local,
        mesh=mesh,
        in_specs=(P(("member", "mp"), None), P(), P(None, "mp"), P("mp"), P("mp", None), P()),
        out_specs=P(("member", "mp"), None),
        check_vma=False,
    )
```

profile of v0, /device:TPU:70, one launch (start us, length us, event | category | flops | bytes accessed | tf_op | source)
XLA Modules:
  0.0 286.0 jit_solution(16125690411349809679)
XLA Ops:
  6.5 0.0 all-gather.2.cloned.1.call-start
  6.6 1.2 convert_reduce_fusion
  7.8 1.3 fusion.10
  9.1 2.1 fusion.12
  11.2 0.1 all-gather.2.cloned.1.call-update
  11.3 0.1 reduce-scatter.2.cloned.1.call-start
  11.4 109.1 %all-gather.2.cloned.1.call-done = bf16[2048,4096]{1,0:T(8,128)(2,1)} async-done(((bf16[64,4096]{1,0:T(8,128)(2,1)}), bf16[2048,4096]{1,0:T(8,128)(2,1)}) %all-gather.2.cloned.1.call-update) | async-done | bytes 16777232 | tf_op jit(solution)/shard_map/all_gather | solution.py:18
  120.5 26.3 %convolution_convert_fusion = bf16[2048,4096]{1,0:T(8,128)(2,1)} fusion(bf16[512,4096]{1,0:T(8,128)(2,1)} %param.10, bf16[2048,4096]{1,0:T(8,128)(2,1)} %all-gather.2.cloned.1.call-done, bf16[4096,512]{1,0:T(8,128)(2,1)} %param.8, f32[512]{0:T(512)} %param.9), kind=kOutput, calls=%fused_computation | convolution fusion | flops 17198743552 | bytes 41945088 | tf_op jit(solution)/shard_map/dot_general | solution.py:26
  146.8 0.0 copy-start
  146.8 0.0 copy-start.1
  146.8 0.1 reduce-scatter.2.cloned.1.call-update
  146.9 130.3 %reduce-scatter.2.cloned.1.call-done = bf16[64,4096]{1,0:T(8,128)(2,1)} async-done(((bf16[2048,4096]{1,0:T(8,128)(2,1)}), bf16[64,4096]{1,0:T(8,128)(2,1)}) %reduce-scatter.2.cloned.1.call-update) | async-done | bytes 524304 | tf_op jit(solution)/shard_map/reduce_scatter | solution.py:25
  277.2 0.0 copy-done
  277.2 0.0 copy-done.1
  277.2 2.0 fusion.14
  (2 shorter events, 0.0 us)
Async XLA Ops:
  6.5 113.9 %all-gather.2.cloned.1.call-start = ((), (), s32[]{:S(2)}) async-start(), calls=%async_computation.1 | async-start | bytes 17301504 | tf_op jit(solution)/shard_map/all_gather | solution.py:18
  11.3 265.9 %reduce-scatter.2.cloned.1.call-start = ((), (), s32[]{:S(2)}) async-start(), calls=%async_computation.2 | async-start | bytes 17301504 | tf_op jit(solution)/shard_map/reduce_scatter | solution.py:25
  146.8 130.4 %copy-start = (bf16[64,4096]{1,0:T(8,128)(2,1)S(1)}, bf16[64,4096]{1,0:T(8,128)(2,1)}, u32[]{:S(2)}) copy-start(bf16[64,4096]{1,0:T(8,128)(2,1)} %param.6) | copy-start | bytes 1572868
  146.8 130.4 %copy-start.1 = (f32[4096]{0:T(1024)S(1)}, f32[4096]{0:T(1024)}, u32[]{:S(2)}) copy-start(f32[4096]{0:T(1024)} %param.11) | copy-start | bytes 49156
Sparse Core Ops, SparseCore 0:
  11.4 109.0 all-gather.1
  147.0 130.1 reduce-scatter.1
where the time goes:
time: 286 us
  waiting for transfers between devices  240 us (84%)
  matrix products  26.3 us (9%)
  between operations  13.4 us (5%)
  other arithmetic  6.63 us (2%)
    reduce_scatter x1, waiting for transfers between devices, local(): lax.psum_scatter(jnp.dot(gathered, w_out, preferred_element_type=jnp.floa...  130 us
    all_gather x1, waiting for transfers between devices, local(): lax.all_gather(source, 'mp', axis=0, tiled=True)  109 us
    dot_general x1, matrix products, local(): jnp.dot(gathered, w_out, preferred_element_type=jnp.float32)  26.3 us
  transfers between devices with their start and end apart: 2, of which 2 were waited for; matrix products, arithmetic and copies ran while one was open for 0% of the time, Pallas kernels for 0%

commit v1 on v0

v1 whole, which is shorter than its diff:
```python
import functools
import math

import jax
import jax.numpy as jnp
from jax import lax
from jax.experimental import pallas as pl
from jax.experimental.pallas import tpu as pltpu
from jax.sharding import PartitionSpec as P

MESH = pl.DeviceIdType.MESH
WAVES = 2
PARTS = 2
PIECES = 4
RIGHT, LEFT = 0, 1
GATHER, SCATTER = 0, 1


def gelu(v):
    return 0.5 * v * (1.0 + jnp.tanh(math.sqrt(2.0 / math.pi) * (v + 0.044715 * (v * v * v))))


def kernel(
    devices, nodes_hbm, gain_hbm, w_in_hbm, b_in_hbm, w_out_hbm, b_out_hbm, out,
    nodes, gain, b_in, b_out, w_in, w_out, rows, hidden, partial, sums,
    load_sem, swap_send, swap_recv, send_sem, recv_sem,
):
    ring = devices // 2
    half = ring // 2
    _, _, _, height, width = rows.shape
    depth = width * PARTS
    units = w_in.shape[2]

    me = lax.axis_index("mp")
    core = lax.rem(me, 2)
    sibling = me + 1 - 2 * core
    to = (lax.rem(me + 2, devices), lax.rem(me + devices - 2, devices))

    def cols(q):
        return pl.ds(q * width, width)

    def hops(q, d):
        return half if (q < PARTS // 2) == (d == RIGHT) else half - 1

    def from_behind(k, d):
        return k if d == RIGHT else lax.rem(ring - k, ring)

    def ahead(j, d):
        return lax.rem(ring - j, ring) if d == RIGHT else j

    def gather_copy(w, k, q, d):
        return pltpu.make_async_remote_copy(
            src_ref=rows.at[w, from_behind(k - 1, d), q],
            dst_ref=rows.at[w, from_behind(k, d), q],
            send_sem=send_sem.at[GATHER, w, d, q, lax.rem(k, 2)],
            recv_sem=recv_sem.at[GATHER, w, d, q, k - 1],
            device_id={"mp": to[d]},
            device_id_type=MESH,
        )

    def scatter_copy(w, k, q, d, first=False):
        j = hops(q, d) + 1 - k
        source = partial.at[w, ahead(j, d), q] if first else sums.at[w, d, j, q]
        return pltpu.make_async_remote_copy(
            src_ref=source,
            dst_ref=sums.at[w, d, j - 1, q],
            send_sem=send_sem.at[SCATTER, w, d, q, lax.rem(k, 2)],
            recv_sem=recv_sem.at[SCATTER, w, d, q, k - 1],
            device_id={"mp": to[d]},
            device_id_type=MESH,
        )

    def begin(phase, w):
        for q in range(PARTS):
            for d in (RIGHT, LEFT):
                if phase == GATHER:
                    gather_copy(w, 1, q, d).start()
                else:
                    scatter_copy(w, 1, q, d, first=True).start()

    def finish_rows(w, q):
        lines = slice(w * height, (w + 1) * height)
        total = (
            nodes[lines, cols(q)].astype(jnp.float32)
            + partial[w, 0, q].astype(jnp.float32)
            + sums[w, RIGHT, 0, q].astype(jnp.float32)
            + sums[w, LEFT, 0, q].astype(jnp.float32)
            + b_out[:, cols(q)]
        )
        out[lines, cols(q)] = total.astype(out.dtype)

    def events(phase, w, k, work=None):
        static = isinstance(k, int)
        for q in range(PARTS):
            for d in (RIGHT, LEFT):
                last = hops(q, d)
                if static and k > last:
                    continue
                copy = gather_copy if phase == GATHER else scatter_copy
                if phase == SCATTER and static and k == 1:
                    copy = functools.partial(scatter_copy, first=True)
                copy(w, k, q, d).wait_recv()
                if static and k == last:
                    if phase == SCATTER and last == half:
                        finish_rows(w, q)
                else:
                    if phase == SCATTER:
                        j = last - k
                        sums[w, d, j, q] = (
                            sums[w, d, j, q].astype(jnp.float32)
                            + partial[w, ahead(j, d), q].astype(jnp.float32)
                        ).astype(sums.dtype)
                    if not static or k > 1:
                        wait_sent(phase, w, k - 1, q, d)
                    copy = gather_copy if phase == GATHER else scatter_copy
                    copy(w, k + 1, q, d).start()
            if work is not None:
                for n in range(q * PIECES // PARTS, (q + 1) * PIECES // PARTS):
                    work(n)

    def wait_sent(phase, w, k, q, d):
        if phase == GATHER:
            gather_copy(w, k, q, d).wait_send()
        else:
            scatter_copy(w, k, q, d, first=True).wait_send()

    def drain(phase, w):
        for q in range(PARTS):
            for d in (RIGHT, LEFT):
                for k in (hops(q, d) - 1, hops(q, d)):
                    wait_sent(phase, w, k, q, d)

    def loop(low, high, body):
        def step(k, carry):
            body(k)
            return carry

        lax.fori_loop(low, high, step, 0)

    slots = ring // 2
    band = slots * height
    tile = 2 * units // PIECES
    step = depth // (2 * PIECES)

    def first_layer(w, m, n):
        h, c = divmod(n * tile, units)
        pre = b_in[h, :, c : c + tile]
        for q in range(PARTS):
            x = rows[w, pl.ds(m * slots, slots), q].reshape(band, width)
            pre = pre + jnp.dot(
                x, w_in[h, q * width : (q + 1) * width, c : c + tile], preferred_element_type=jnp.float32
            )
        hidden[pl.ds(m * band, band), n * tile : (n + 1) * tile] = gelu(pre).astype(hidden.dtype)

    def second_layer(w, m, n):
        x = hidden[pl.ds(m * band, band), :]
        for c in (2 * n * step, (2 * n + 1) * step):
            share = jnp.dot(
                x,
                w_out[:, :, c : c + step].reshape(2 * units, step),
                preferred_element_type=jnp.float32,
            )
            q, c = divmod(c, width)
            partial[w, pl.ds(m * slots, slots), q, :, c : c + step] = share.reshape(
                slots, height, step
            ).astype(partial.dtype)

    def normalize(w):
        for r in range(height // 16):
            lines = slice(w * height + r * 16, w * height + (r + 1) * 16)
            values = nodes[lines, :].astype(jnp.float32)
            mean = jnp.mean(values, axis=1, keepdims=True)
            centred = values - mean
            var = jnp.mean(centred * centred, axis=1, keepdims=True)
            scaled = (centred * lax.rsqrt(var + 1e-05) * gain[...]).astype(rows.dtype)
            for q in range(PARTS):
                rows[w, 0, q, r * 16 : (r + 1) * 16, :] = scaled[:, q * width : (q + 1) * width]

    loads = [
        pltpu.make_async_copy(source, target, load_sem.at[i])
        for i, (source, target) in enumerate(
            (
                (nodes_hbm.at[:height], nodes.at[:height]),
                (gain_hbm, gain),
                (nodes_hbm.at[height:], nodes.at[height:]),
                (b_in_hbm, b_in.at[0]),
                (b_out_hbm, b_out),
                (w_in_hbm, w_in.at[0]),
                (w_out_hbm, w_out.at[0]),
            )
        )
    ]
    swaps = [
        pltpu.make_async_remote_copy(
            src_ref=source,
            dst_ref=target,
            send_sem=swap_send.at[i],
            recv_sem=swap_recv.at[i],
            device_id={"mp": sibling},
            device_id_type=MESH,
        )
        for i, (source, target) in enumerate(
            ((w_in_hbm, w_in.at[1]), (w_out_hbm, w_out.at[1]), (b_in_hbm, b_in.at[1]))
        )
    ]

    barrier = pltpu.get_barrier_semaphore()
    for other in (*to, sibling):
        pl.semaphore_signal(barrier, inc=1, device_id={"mp": other}, device_id_type=MESH)
    for load in loads:
        load.start()
    loads[0].wait()
    loads[1].wait()
    normalize(0)
    pl.semaphore_wait(barrier, 3)

    begin(GATHER, 0)
    loads[2].wait()
    normalize(1)
    begin(GATHER, 1)
    for swap in swaps:
        swap.start()
    events(GATHER, 0, 1)
    loop(2, half - 1, lambda k: events(GATHER, 0, k))
    events(GATHER, 1, 1)
    events(GATHER, 0, half - 1)
    events(GATHER, 1, 2)
    events(GATHER, 0, half)
    drain(GATHER, 0)
    for load in loads[3:]:
        load.wait()
    for swap in swaps:
        swap.wait()

    def compute_beside(phase, w, compute, k0):
        loop(k0, k0 + 2, lambda k: events(phase, w, k, lambda q: first_layer(compute, k - k0, q)))
        loop(k0 + 2, k0 + 4, lambda k: events(phase, w, k, lambda q: second_layer(compute, k - k0 - 2, q)))
        if k0 + 4 < half - 1:
            loop(k0 + 4, half - 1, lambda k: events(phase, w, k))

    compute_beside(GATHER, 1, 0, 3)
    begin(SCATTER, 0)
    events(GATHER, 1, half - 1)
    events(SCATTER, 0, 1)
    events(GATHER, 1, half)
    drain(GATHER, 1)
    compute_beside(SCATTER, 0, 1, 2)
    begin(SCATTER, 1)
    events(SCATTER, 0, half - 1)
    events(SCATTER, 1, 1)
    events(SCATTER, 0, half)
    drain(SCATTER, 0)
    loop(2, half - 1, lambda k: events(SCATTER, 1, k))
    events(SCATTER, 1, half - 1)
    events(SCATTER, 1, half)
    drain(SCATTER, 1)


def solution(mesh):
    devices = mesh.shape["mp"]

    def local(nodes, norm_gain, w_in, b_in, w_out, b_out):
        total, depth = nodes.shape
        units = w_in.shape[1]
        ring, height = devices // 2, total // WAVES
        half = ring // 2
        bf16, f32 = jnp.bfloat16, jnp.float32
        in_hbm = pl.BlockSpec(memory_space=pltpu.HBM)
        return pl.pallas_call(
            functools.partial(kernel, devices),
            out_shape=jax.ShapeDtypeStruct((total, depth), bf16),
            in_specs=[in_hbm] * 6,
            out_specs=pl.BlockSpec(memory_space=pltpu.VMEM),
            scratch_shapes=[
                pltpu.VMEM((total, depth), bf16),
                pltpu.VMEM((1, depth), f32),
                pltpu.VMEM((2, 1, units), f32),
                pltpu.VMEM((1, depth), f32),
                pltpu.VMEM((2, depth, units), bf16),
                pltpu.VMEM((2, units, depth), bf16),
                pltpu.VMEM((WAVES, ring, PARTS, height, depth // PARTS), bf16),
                pltpu.VMEM((ring * height, 2 * units), bf16),
                pltpu.VMEM((WAVES, ring, PARTS, height, depth // PARTS), bf16),
                pltpu.VMEM((WAVES, 2, half, PARTS, height, depth // PARTS), bf16),
                pltpu.SemaphoreType.DMA((7,)),
                pltpu.SemaphoreType.DMA((3,)),
                pltpu.SemaphoreType.DMA((3,)),
                pltpu.SemaphoreType.DMA((2, WAVES, 2, PARTS, 2)),
                pltpu.SemaphoreType.DMA((2, WAVES, 2, PARTS, half)),
            ],
            compiler_params=pltpu.CompilerParams(
                collective_id=0, has_side_effects=True, vmem_limit_bytes=48 * 2**20
            ),
        )(
            *(
                pltpu.with_memory_space_constraint(x, pltpu.HBM)
                for x in (
                    nodes,
                    norm_gain.reshape(1, depth),
                    w_in,
                    b_in.reshape(1, units),
                    w_out,
                    b_out.reshape(1, depth),
                )
            )
        )

    return jax.shard_map(
        local,
        mesh=mesh,
        in_specs=(P(("member", "mp"), None), P(), P(None, "mp"), P("mp"), P("mp", None), P()),
        out_specs=P(("member", "mp"), None),
        check_vma=False,
    )
```

time: 286 us -> 187 us (0.65)
  waiting for transfers between devices: 240 us -> 0 us
  Pallas kernels: 0 us -> 186 us
  matrix products: 26.3 us -> 0 us
  between operations: 13.4 us -> 0.01 us
  other arithmetic: 6.63 us -> 0 us
    pallas_call x0 -> x1, Pallas kernels: none -> 186 us  [local(): pl.pallas_call(functools.partial(kernel, devices), out_shape=jax.ShapeDty...]
    reduce_scatter x1 -> x0, waiting for transfers between devices: 130 us -> none  [local(): lax.psum_scatter(jnp.dot(gathered, w_out, preferred_element_type=jnp.floa...]
    all_gather x1 -> x0, waiting for transfers between devices: 109 us -> none  [local(): lax.all_gather(source, 'mp', axis=0, tiled=True)]
    dot_general x1 -> x0, matrix products: 26.3 us -> none  [local(): jnp.dot(gathered, w_out, preferred_element_type=jnp.float32)]
    convert_element_type x2 -> x0, other arithmetic: 4.07 us -> none  [the longest x1 2.08 us: normalize(): ((values - mean) / jnp.sqrt(var + 1e-05) * norm_gain).astype(jnp.bfloat16)]
  transfers between devices with their start and end apart: 2 -> 0, of which waited for: 2 -> 0; matrix products, arithmetic and copies ran while one was open for 0% -> 0% of each run, Pallas kernels for 0% -> 0%
where the time goes in v1:
time: 187 us
  Pallas kernels  186 us (99%)
    pallas_call x1, Pallas kernels, local(): pl.pallas_call(functools.partial(kernel, devices), out_shape=jax.ShapeDty...  186 us

profile of v1, /device:TPU:70, one launch (start us, length us, event | category | flops | bytes accessed | tf_op | source)
XLA Modules:
  0.0 187.2 jit_solution(9623702797348129322)
XLA Ops:
  0.0 186.4 %shard_map.64 = bf16[64,4096]{1,0:T(8,128)(2,1)S(1)} custom-call(bf16[64,4096]{1,0:T(8,128)(2,1)} %nodes_hbm.1, f32[1,4096]{1,0:T(1,128)} %bitcast.3, bf16[4096,512]{1,0:T(8,128)(2,1)} %w_in_hbm.1, f32[1,512]{1,0:T(1,128)} %bitcast.5, bf16[512,4096]{1,0:T(8,128)(2,1)} %w_out_hbm.1, f32[1,4096]{1,0:T(1,128)} %bitcast.4), custom_call_target="tpu_custom_call" | custom-call | tf_op jit(solution)/shard_map/pallas_call | solution.py:269
  186.4 0.8 copy.8

commit v2 on v1

--- a/solution.py
+++ b/solution.py
@@ -14,6 +14,7 @@
 PIECES = 4
 RIGHT, LEFT = 0, 1
 GATHER, SCATTER = 0, 1
+ORDER = [pair for i in range(PARTS) for pair in ((i, RIGHT), (PARTS - 1 - i, LEFT))]
 
 
 def gelu(v):
@@ -71,12 +72,11 @@
         )
 
     def begin(phase, w):
-        for q in range(PARTS):
-            for d in (RIGHT, LEFT):
-                if phase == GATHER:
-                    gather_copy(w, 1, q, d).start()
-                else:
-                    scatter_copy(w, 1, q, d, first=True).start()
+        for q, d in ORDER:
+            if phase == GATHER:
+                gather_copy(w, 1, q, d).start()
+            else:
+                scatter_copy(w, 1, q, d, first=True).start()
 
     def finish_rows(w, q):
         lines = slice(w * height, (w + 1) * height)
@@ -91,32 +91,30 @@
 
     def events(phase, w, k, work=None):
         static = isinstance(k, int)
-        for q in range(PARTS):
-            for d in (RIGHT, LEFT):
-                last = hops(q, d)
-                if static and k > last:
-                    continue
+        for i, (q, d) in enumerate(ORDER):
+            last = hops(q, d)
+            if static and k > last:
+                continue
+            copy = gather_copy if phase == GATHER else scatter_copy
+            if phase == SCATTER and static and k == 1:
+                copy = functools.partial(scatter_copy, first=True)
+            copy(w, k, q, d).wait_recv()
+            if static and k == last:
+                if phase == SCATTER and last == half:
+                    finish_rows(w, q)
+            else:
+                if phase == SCATTER:
+                    j = last - k
+                    sums[w, d, j, q] = (
+                        sums[w, d, j, q].astype(jnp.float32)
+                        + partial[w, ahead(j, d), q].astype(jnp.float32)
+                    ).astype(sums.dtype)
+                if not static or k > 1:
+                    wait_sent(phase, w, k - 1, q, d)
                 copy = gather_copy if phase == GATHER else scatter_copy
-                if phase == SCATTER and static and k == 1:
-                    copy = functools.partial(scatter_copy, first=True)
-                copy(w, k, q, d).wait_recv()
-                if static and k == last:
-                    if phase == SCATTER and last == half:
-                        finish_rows(w, q)
-                else:
-                    if phase == SCATTER:
-                        j = last - k
-                        sums[w, d, j, q] = (
-                            sums[w, d, j, q].astype(jnp.float32)
-                            + partial[w, ahead(j, d), q].astype(jnp.float32)
-                        ).astype(sums.dtype)
-                    if not static or k > 1:
-                        wait_sent(phase, w, k - 1, q, d)
-                    copy = gather_copy if phase == GATHER else scatter_copy
-                    copy(w, k + 1, q, d).start()
-            if work is not None:
-                for n in range(q * PIECES // PARTS, (q + 1) * PIECES // PARTS):
-                    work(n)
+                copy(w, k + 1, q, d).start()
+            if work is not None and i % (len(ORDER) // PIECES) == 0:
+                work(i * PIECES // len(ORDER))
 
     def wait_sent(phase, w, k, q, d):
         if phase == GATHER:

time: 187 us -> 186 us (level)
  no operation moved by 1% of the time
where the time goes in v2:
time: 186 us
  Pallas kernels  185 us (99%)
    pallas_call x1, Pallas kernels, local(): pl.pallas_call(functools.partial(kernel, devices), out_shape=jax.ShapeDty...  185 us

profile of v2, /device:TPU:70, one launch (start us, length us, event | category | flops | bytes accessed | tf_op | source)
XLA Modules:
  0.0 185.7 jit_solution(18260018664827541301)
XLA Ops:
  0.0 184.9 %shard_map.64 = bf16[64,4096]{1,0:T(8,128)(2,1)S(1)} custom-call(bf16[64,4096]{1,0:T(8,128)(2,1)} %nodes_hbm.1, f32[1,4096]{1,0:T(1,128)} %bitcast.3, bf16[4096,512]{1,0:T(8,128)(2,1)} %w_in_hbm.1, f32[1,512]{1,0:T(1,128)} %bitcast.5, bf16[512,4096]{1,0:T(8,128)(2,1)} %w_out_hbm.1, f32[1,4096]{1,0:T(1,128)} %bitcast.4), custom_call_target="tpu_custom_call" | custom-call | tf_op jit(solution)/shard_map/pallas_call | solution.py:267
  185.0 0.8 copy.8
